TPU v7x, 512 devices: a 8x2x16 block of a 8x8x16 slice. The times are simulated.
512 devices in a mesh: groups: 2 (over y), ctx: 32 (over z, core), tp: 8 (over x).
Axes of the slice: x: 8, y: 2, z: 16, core: 2. Of those that a mesh axis runs over, the one named last changes fastest.
The devices are a block of a 8x8x16 slice.
Arguments:
- query_matrix: bfloat16 [8192, 8192], P(('groups', 'ctx'), 'tp'), parts along dimension 0, may hold values from -20 to 20
- key_matrix: bfloat16 [8192, 1024], P(('groups', 'ctx'), 'tp'), parts along dimension 0, may hold values from -20 to 20
- value_matrix: bfloat16 [8192, 1024], P(('groups', 'ctx'), 'tp'), parts along dimension 0, may hold values from -6 to 6
- doc_ids: int32 [8192], P('groups'), parts along dimension 0, may hold values from 0 to 5, never falling along the last dimension, each value on 1 to 2048 neighbouring positions
- out_weight: bfloat16 [8192, 4096], P('tp', 'ctx'), may hold values from -0.0625 to 0.0625
Outputs:
- projected: bfloat16 [8192, 4096], P(('groups', 'ctx'), 'tp'), parts along dimension 0
There are 2 independent parts, one for each index of `groups`. A program takes and returns all parts, laid end to end along the dimension named above; an argument that names none is the same for every part. Nothing has to cross between parts.
Inputs may be any that keep to these rules, and one draw needn't show every extreme that they name: `doc_ids`: non-decreasing along the sequence; each document holds 1 to 2048 tokens, one exactly 2048.
All inputs are finite; a program needn't handle non-finite values.
Results may differ from a plain program's by a relative error of at most 0.015.
Values may be sent and summed in bfloat16 or wider, within the bound.
No kernel may reach another device: no remote copies, remote signals or barrier semaphores. Data moves between devices by JAX's collectives and lax.ppermute only.
A program may use at most 64 MiB of HBM per device.

v0:
```python
import math
import jax
import jax.numpy as jnp
from jax import lax
from jax.sharding import PartitionSpec as P

HEAD_SIZE = 128
rope_base = 1000000.0


def in_one_piece(arrays, axis, dim, along):
    ends, at = ([], 0)
    for a in arrays[:-1]:
        at += a.shape[along]
        ends.append(at)
    both = jnp.concatenate(arrays, axis=along)
    return tuple(jnp.split(lax.all_gather(both, axis, axis=dim, tiled=True), ends, axis=along))


def split_up(x, dim, size):
    lengths = x.shape
    pieces = x.reshape(*lengths[:dim], size, lengths[dim] // size, *lengths[dim + 1 :])
    return jnp.moveaxis(pieces, dim, 0)


def sent_and_summed(x, axis, dim):
    pieces = split_up(x, dim, lax.axis_size(axis))
    arrived = lax.all_to_all(pieces, axis, split_axis=0, concat_axis=0, tiled=True)
    return arrived.astype(jnp.float32).sum(axis=0)


def rotary_tables(rows, token_positions, heads):
    half_dim = HEAD_SIZE // 2
    frequency = jnp.power(
        jnp.float32(rope_base), -jnp.arange(half_dim, dtype=jnp.float32) * (2.0 / HEAD_SIZE)
    )
    angles = token_positions.astype(jnp.float32)[:, None] * frequency[None, :]
    cosine = jnp.cos(angles)[:, None, :]
    sine = jnp.sin(angles)[:, None, :]
    values = rows.astype(jnp.float32).reshape(rows.shape[0], heads, HEAD_SIZE)
    first = values[..., :half_dim]
    second = values[..., half_dim:]
    turned = jnp.concatenate([first * cosine - second * sine, second * cosine + first * sine], -1)
    return turned.reshape(rows.shape[0], heads * HEAD_SIZE).astype(jnp.bfloat16)


def keep_state(held_state, unused_block):
    return held_state


def on_device(query_matrix, key_matrix, value_matrix, doc_ids, out_weight):
    ctx_index = lax.axis_index("ctx")
    tok_rows = query_matrix.shape[0]
    query_heads = query_matrix.shape[1] // HEAD_SIZE
    key_heads = key_matrix.shape[1] // HEAD_SIZE
    group_width = query_heads // key_heads
    inverse_root = HEAD_SIZE ** (-0.5)
    local_rows = jnp.arange(tok_rows, dtype=jnp.int32)
    given_pos = ctx_index * tok_rows + local_rows
    query_matrix_rot = rotary_tables(query_matrix, given_pos, query_heads)
    keys_here = rotary_tables(key_matrix, given_pos, key_heads)
    query_doc = jnp.take(doc_ids, given_pos, axis=0)
    query_four = query_matrix_rot.reshape(tok_rows, key_heads, group_width, HEAD_SIZE)
    first_doc = jnp.min(query_doc)
    last_doc = jnp.max(query_doc)
    last_pos = jnp.max(given_pos)

    def attend(state, block):
        key_block, value_block, doc_block, pos_block = block
        row_max, totals, accum = state
        scores = (
            jnp.einsum("qkgd,skd->kgqs", query_four, key_block, preferred_element_type=jnp.float32)
            * inverse_root
        )
        allowed = (
            (query_doc[:, None] == doc_block[None, :]) & (pos_block[None, :] <= given_pos[:, None])
        )[None, None]
        new_max = jnp.maximum(row_max, jnp.max(jnp.where(allowed, scores, -1e30), -1))
        weights = jnp.where(allowed, jnp.exp(scores - new_max[..., None]), 0.0)
        factor = jnp.exp(row_max - new_max)
        totals = totals * factor + jnp.sum(weights, -1)
        accum = accum * jnp.transpose(factor, (2, 0, 1))[..., None] + jnp.einsum(
            "kgqs,skd->qkgd",
            weights.astype(jnp.bfloat16),
            value_block,
            preferred_element_type=jnp.float32,
        )
        return (new_max, totals, accum)

    start_state = (
        jnp.full((key_heads, group_width, tok_rows), -1e30, jnp.float32),
        jnp.zeros((key_heads, group_width, tok_rows), jnp.float32),
        jnp.zeros((tok_rows, key_heads, group_width, HEAD_SIZE), jnp.float32),
    )
    key_piece, value_piece = in_one_piece((keys_here, value_matrix), "ctx", 0, 1)
    count = key_piece.shape[0]
    block_rows = math.gcd(count, 512)
    block_count = count // block_rows
    positions = jnp.arange(count, dtype=jnp.int32)
    blocks = (
        key_piece.reshape(block_count, block_rows, key_heads, HEAD_SIZE),
        value_piece.reshape(block_count, block_rows, key_heads, HEAD_SIZE),
        jnp.take(doc_ids, positions, axis=0).reshape(block_count, block_rows),
        positions.reshape(block_count, block_rows),
    )

    def step_block(inner_state, block):
        live = (
            (jnp.min(block[3]) <= last_pos)
            & (jnp.min(block[2]) <= last_doc)
            & (jnp.max(block[2]) >= first_doc)
        )
        return (lax.cond(live, attend, keep_state, inner_state, block), None)

    final_state, unused_out = lax.scan(step_block, start_state, blocks)
    row_max, totals, accum = final_state
    attention = (
        (accum / jnp.transpose(totals, (2, 0, 1))[..., None])
        .reshape(tok_rows, query_heads * HEAD_SIZE)
        .astype(jnp.bfloat16)
    )
    terms = jnp.dot(
        attention,
        lax.all_gather(out_weight, "ctx", axis=1, tiled=True),
        preferred_element_type=jnp.float32,
    )
    return sent_and_summed(terms.astype(jnp.bfloat16), "tp", 1).astype(jnp.bfloat16)


def solution(mesh):
    in_specs = (
        P(("groups", "ctx"), "tp"),
        P(("groups", "ctx"), "tp"),
        P(("groups", "ctx"), "tp"),
        P("groups"),
        P("tp", "ctx"),
    )
    out_specs = P(("groups", "ctx"), "tp")
    return jax.shard_map(
        on_device, mesh=mesh, in_specs=in_specs, out_specs=out_specs, check_vma=False
    )
```

profile of v0, /device:TPU:65, one launch (start us, length us, event | category | flops | bytes accessed | tf_op | source)
XLA Modules:
  0.0 262.6 jit_solution(11426903617318993670)
XLA Ops:
  6.6 0.6 fusion.36
  7.2 0.9 copy.19
  8.1 0.9 copy.20
  8.9 0.2 fusion.32
  9.2 0.6 pad_maximum_fusion.1
  9.9 0.7 all-gather.5.cloned.1.call-update
  10.7 1.1 copy.21
  12.4 1.1 gather_fusion.1
  13.5 23.0 %gather_fusion = s32[4096]{0:T(1024)S(1)} fusion(s32[4096]{0:T(1024)S(1)} %copy-done, s32[4096]{0:T(1024)S(1)} %iota_clamp_fusion), kind=kCustom, calls=%fused_computation | custom fusion | bytes 49152 | tf_op jit(solution)/shard_map/jit(_take)/gather | solution.py:103
  36.6 0.7 fusion.39
  37.3 82.9 %all-gather.3.cloned.1.call-done = bf16[4096,256]{0,1:T(8,128)(2,1)} async-done(((bf16[128,256]{0,1:T(8,128)(2,1)}), bf16[4096,256]{0,1:T(8,128)(2,1)}) %all-gather.3.cloned.1.call-update) | async-done | bytes 2097168 | tf_op jit(solution)/shard_map/all_gather | solution.py:17
  120.2 1.7 fusion.41
  121.9 0.7 copy.22
  122.6 0.5 copy.25
  123.1 0.7 copy.28
  123.8 37.2 %while.15 = (s32[]{:T(128)}, f32[1,8,128]{2,1,0:T(8,128)S(1)}, f32[1,8,128]{2,1,0:T(8,128)S(1)}, f32[128,1,8,128]{0,3,2,1:T(8,128)S(1)}, s32[8,512]{1,0:T(8,128)...) while((s32[]{:T(128)}, f32[1,8,128]{2,1,0:T(8,128)S(1)}, ...), condition=%wide.region_11.12_spmd.clone, body=%wide.region_3.11_spmd.clone.sunk | while | flops 274666112 | bytes 8207207 | solution.py:115
  123.9 0.7 fusion.45
  128.2 1.8 conditional.3
  128.5 0.5 fusion.2
  129.0 0.4 fusion.6
  129.4 0.6 fusion.7
  130.1 0.7 fusion.45
  134.5 0.7 fusion.45
  138.9 0.7 fusion.45
  143.3 0.7 fusion.45
  147.8 0.7 fusion.45
  152.2 0.7 fusion.45
  156.6 0.7 fusion.45
  161.1 54.5 %all-gather.5.cloned.1.call-done = bf16[1024,4096]{1,0:T(8,128)(2,1)} async-done(((bf16[1024,128]{1,0:T(8,128)(2,1)}), bf16[1024,4096]{1,0:T(8,128)(2,1)}) %all-gather.5.cloned.1.call-update) | async-done | bytes 8388624 | tf_op jit(solution)/shard_map/all_gather | solution.py:124
  215.6 4.7 %convolution_convert_fusion = bf16[128,4096]{1,0:T(8,128)(2,1)S(1)} fusion(bf16[128,1024]{0,1:T(8,128)(2,1)S(1)} %bitcast.90, bf16[1024,4096]{1,0:T(8,128)(2,1)} %all-gather.5.cloned.1.call-done), kind=kOutput, calls=%fused_computation.35 | convolution fusion | flops 1074266112 | bytes 9699328 | tf_op jit(solution)/shard_map/dot_general | solution.py:122
  220.3 34.6 %all_to_all.5 = bf16[8,128,512]{2,1,0:T(8,128)(2,1)S(1)} all-to-all(bf16[8,128,512]{2,1,0:T(8,128)(2,1)S(1)} %bitcast.85), channel_id=1, replica_groups=mesh['groups'=2,'ctx'=32,'tp'=8] {'tp'}, dimensions={0} | all-to-all | bytes 2097152 | tf_op jit(solution)/shard_map/all_to_all | solution.py:28
  254.9 0.8 reduce_sum.23
  (43 shorter events, 1.2 us)
Async XLA Ops:
  6.5 5.8 %copy-start = (s32[4096]{0:T(1024)S(1)}, s32[4096]{0:T(1024)}, u32[]{:S(2)}) copy-start(s32[4096]{0:T(1024)} %param.12) | copy-start | bytes 49156
  6.6 113.7 %all-gather.3.cloned.1.call-start = ((), (), s32[]{:S(2)}) async-start(), calls=%async_computation.1 | async-start | bytes 2162688 | tf_op jit(solution)/shard_map/all_gather | solution.py:17
  9.9 205.7 %all-gather.5.cloned.1.call-start = ((), (), s32[]{:S(2)}) async-start(), calls=%async_computation.2 | async-start | bytes 8650752 | tf_op jit(solution)/shard_map/all_gather | solution.py:124
Sparse Core Ops, SparseCore 0:
  10.0 110.2 all-gather.2
  122.3 93.2 all-gather.4
where the time goes:
time: 263 us
  waiting for transfers between devices  138 us (52%)
  blocking collectives  34.6 us (13%)
  local copies, waits for them, and re-layouts  30.9 us (12%)
  loops' own time  29.9 us (11%)
  between operations  13.6 us (5%)
  other arithmetic  9.57 us (4%)
  matrix products  5.76 us (2%)
    all_gather x1, waiting for transfers between devices, in_one_piece(): lax.all_gather(both, axis, axis=dim, tiled=True)  82.9 us
    all_gather x1, waiting for transfers between devices, on_device(): lax.all_gather(out_weight, 'ctx', axis=1, tiled=True)  54.5 us
    all_to_all x1, blocking collectives, sent_and_summed(): lax.all_to_all(pieces, axis, split_axis=0, concat_axis=0, tiled=True)  34.6 us
    another operation x1, loops' own time, on_device(): final_state, unused_out = lax.scan(step_block, start_state, blocks)  29.7 us
    gather x2, local copies, waits for them, and re-layouts, on_device(): jnp.take(doc_ids, positions, axis=0).reshape(block_count, block_rows)  23 us
    reduce_max x8, other arithmetic, step_block(): jnp.max(block[2]) >= first_doc  5.52 us
  transfers between devices with their start and end apart: 2, of which 2 were waited for; matrix products, arithmetic and copies ran while one was open for 14% of the time, Pallas kernels for 0%

commit v1 on v0

--- a/solution.py
+++ b/solution.py
@@ -1,3 +1,4 @@
+import functools
 import math
 import jax
 import jax.numpy as jnp
@@ -6,6 +7,14 @@
 
 HEAD_SIZE = 128
 rope_base = 1000000.0
+
+
+def case_cover(vec, mesh_ax):
+    taken_in = jnp.concatenate(lax.psum(1, mesh_ax) * [vec], axis=1)
+    return lax.all_to_all(taken_in, mesh_ax, 1, 1, tiled=True)
+
+
+show_ratios = functools.partial(case_cover, mesh_ax="ctx")
 
 
 def in_one_piece(arrays, axis, dim, along):
@@ -119,11 +128,7 @@
         .reshape(tok_rows, query_heads * HEAD_SIZE)
         .astype(jnp.bfloat16)
     )
-    terms = jnp.dot(
-        attention,
-        lax.all_gather(out_weight, "ctx", axis=1, tiled=True),
-        preferred_element_type=jnp.float32,
-    )
+    terms = jnp.dot(attention, show_ratios(out_weight), preferred_element_type=jnp.float32)
     return sent_and_summed(terms.astype(jnp.bfloat16), "tp", 1).astype(jnp.bfloat16)
 
 

time: 263 us -> 508 us (1.93); the launches traced: 263 us -> 500 us
  waiting for transfers between devices: 138 us -> 302 us
  starting transfers between devices: 0.07 us -> 46.4 us
  local copies, waits for them, and re-layouts: 30.9 us -> 57.1 us
    all_to_all x0 -> x1, waiting for transfers between devices: none -> 176 us  [case_cover(): return lax.all_to_all(taken_in, mesh_ax, 1, 1, tiled=True)]
    all_gather x1 -> x0, waiting for transfers between devices: 54.5 us -> none  [on_device(): lax.all_gather(out_weight, 'ctx', axis=1, tiled=True)]
    all_to_all x0 -> x1, starting transfers between devices: none -> 46.3 us  [case_cover(): return lax.all_to_all(taken_in, mesh_ax, 1, 1, tiled=True)]
    all_gather x1, waiting for transfers between devices: 82.9 us -> 126 us  [in_one_piece(): lax.all_gather(both, axis, axis=dim, tiled=True)]
    all_to_all x0 -> x2, local copies, waits for them, and re-layouts: none -> 23.7 us  [case_cover(): return lax.all_to_all(taken_in, mesh_ax, 1, 1, tiled=True)]
  transfers between devices with their start and end apart: 2 -> 2, of which waited for: 2 -> 2; matrix products, arithmetic and copies ran while one was open for 14% -> 8% of each run, Pallas kernels for 0% -> 0%
where the time goes in v1:
time: 508 us; the launch traced here: 500 us
  waiting for transfers between devices  302 us (59%)
  local copies, waits for them, and re-layouts  57.1 us (11%)
  starting transfers between devices  46.4 us (9%)
  blocking collectives  33.7 us (7%)
  loops' own time  29.9 us (6%)
  between operations  13.9 us (3%)
  other arithmetic  10.1 us (2%)
  matrix products  7.37 us (1%)
    all_to_all x1, waiting for transfers between devices, case_cover(): return lax.all_to_all(taken_in, mesh_ax, 1, 1, tiled=True)  176 us
    all_gather x1, waiting for transfers between devices, in_one_piece(): lax.all_gather(both, axis, axis=dim, tiled=True)  126 us
    all_to_all x1, starting transfers between devices, case_cover(): return lax.all_to_all(taken_in, mesh_ax, 1, 1, tiled=True)  46.3 us
    all_to_all x1, blocking collectives, sent_and_summed(): lax.all_to_all(pieces, axis, split_axis=0, concat_axis=0, tiled=True)  33.7 us
    another operation x1, loops' own time, on_device(): final_state, unused_out = lax.scan(step_block, start_state, blocks)  29.7 us
    all_to_all x2, local copies, waits for them, and re-layouts, case_cover(): return lax.all_to_all(taken_in, mesh_ax, 1, 1, tiled=True)  23.7 us
    gather x2, local copies, waits for them, and re-layouts, on_device(): jnp.take(doc_ids, positions, axis=0).reshape(block_count, block_rows)  23 us
  transfers between devices with their start and end apart: 2, of which 2 were waited for; matrix products, arithmetic and copies ran while one was open for 8% of the time, Pallas kernels for 0%

profile of v1, /device:TPU:65, one launch (start us, length us, event | category | flops | bytes accessed | tf_op | source)
XLA Modules:
  0.0 500.2 jit_solution(14058825310169833204)
XLA Ops:
  6.6 1.1 copy.66
  8.5 3.2 copy-done.1
  11.8 11.9 %copy.98 = bf16[1024,32,128]{2,0,1:T(8,128)(2,1)} copy(bf16[1024,32,128]{0,2,1:T(8,128)(2,1)} %bitcast.87) | data formatting | bytes 16777216 | tf_op jit(solution)/shard_map/all_to_all | solution.py:14
  23.6 46.3 %all-to-all-start = ((bf16[1024,32,128]{2,0,1:T(8,128)(2,1)}), bf16[1024,32,128]{2,0,1:T(8,128)(2,1)}, u32[]{:S(2)}, u32[]{:S(2)}) async-start(bf16[1024,32,128]{2,0,1:T(8,128)(2,1)} %copy.98), calls=%async_computation | async-start | bytes 16777216 | tf_op jit(solution)/shard_map/all_to_all | solution.py:14
  70.3 0.6 fusion.36
  71.2 0.6 pad_maximum_fusion.1
  72.6 1.1 gather_fusion.1
  73.8 23.0 %gather_fusion = s32[4096]{0:T(1024)S(1)} fusion(s32[4096]{0:T(1024)S(1)} %copy-done, s32[4096]{0:T(1024)S(1)} %iota_clamp_fusion), kind=kCustom, calls=%fused_computation | custom fusion | bytes 49152 | tf_op jit(solution)/shard_map/jit(_take)/gather | solution.py:112
  96.8 0.6 fusion.39
  97.5 125.6 %all-gather.2.cloned.1.call-done = bf16[4096,256]{0,1:T(8,128)(2,1)} async-done(((bf16[128,256]{0,1:T(8,128)(2,1)}), bf16[4096,256]{0,1:T(8,128)(2,1)}) %all-gather.2.cloned.1.call-update) | async-done | bytes 2097168 | tf_op jit(solution)/shard_map/all_gather | solution.py:26
  223.1 1.7 fusion.41
  224.7 0.7 copy.62
  225.4 0.5 copy.65
  225.9 0.7 copy.102
  226.7 37.7 %while.15 = (s32[]{:T(128)}, f32[1,8,128]{2,1,0:T(8,128)S(1)}, f32[1,8,128]{2,1,0:T(8,128)S(1)}, f32[128,1,8,128]{0,3,2,1:T(8,128)S(1)}, s32[8,512]{1,0:T(8,128)...) while((s32[]{:T(128)}, f32[1,8,128]{2,1,0:T(8,128)S(1)}, ...), condition=%wide.region_11.12_spmd.clone, body=%wide.region_3.11_spmd.clone.sunk | while | flops 274666112 | bytes 8207207 | solution.py:124
  226.7 0.8 fusion.45
  231.1 1.8 conditional.3
  231.4 0.5 fusion.2
  231.9 0.4 fusion.6
  232.3 0.6 fusion.7
  233.0 0.8 fusion.45
  237.5 0.8 fusion.45
  242.0 0.8 fusion.45
  246.5 0.8 fusion.45
  250.9 0.8 fusion.45
  255.4 0.8 fusion.45
  259.9 0.8 fusion.45
  264.5 176.1 %all-to-all-done = bf16[1024,32,128]{2,0,1:T(8,128)(2,1)} async-done(((bf16[1024,32,128]{2,0,1:T(8,128)(2,1)}), bf16[1024,32,128]{2,0,1:T(8,128)(2,1)}, u32[]{:S(2)}, u32[]{:S(2)}) %all-to-all-start) | async-done | bytes 8388640 | tf_op jit(solution)/shard_map/all_to_all | solution.py:14
  440.6 11.9 %copy.99 = bf16[1024,32,128]{0,2,1:T(8,128)(2,1)} copy(bf16[1024,32,128]{2,0,1:T(8,128)(2,1)} %all-to-all-done) | data formatting | bytes 16777216 | tf_op jit(solution)/shard_map/all_to_all | solution.py:14
  452.4 6.3 %convolution_convert_fusion = bf16[128,4096]{1,0:T(8,128)(2,1)S(1)} fusion(bf16[128,1024]{0,1:T(8,128)(2,1)S(1)} %bitcast.94, bf16[1024,4096]{0,1:T(8,128)(2,1)} %bitcast.86), kind=kOutput, calls=%fused_computation.35 | convolution fusion | flops 1074266112 | bytes 9699328 | tf_op jit(solution)/shard_map/dot_general | solution.py:131
  458.8 33.7 %all_to_all.17 = bf16[8,128,512]{2,1,0:T(8,128)(2,1)S(1)} all-to-all(bf16[8,128,512]{2,1,0:T(8,128)(2,1)S(1)} %bitcast.90), channel_id=1, replica_groups=mesh['groups'=2,'ctx'=32,'tp'=8] {'tp'}, dimensions={0} | all-to-all | bytes 2097152 | tf_op jit(solution)/shard_map/all_to_all | solution.py:37
  492.5 0.8 reduce_sum.23
  (85 shorter events, 2.4 us)
Async XLA Ops:
  6.5 66.1 %copy-start = (s32[4096]{0:T(1024)S(1)}, s32[4096]{0:T(1024)}, u32[]{:S(2)}) copy-start(s32[4096]{0:T(1024)} %param.12) | copy-start | bytes 49156
  8.5 3.2 copy-start.1
  23.6 46.4 %copy-start.3 = (bf16[128,128]{1,0:T(8,128)(2,1)S(1)}, bf16[128,128]{1,0:T(8,128)(2,1)}, u32[]{:S(2)}) copy-start(bf16[128,128]{1,0:T(8,128)(2,1)} %param.10) | copy-start | bytes 98308
  23.6 46.5 %copy-start.4 = (bf16[128,128]{1,0:T(8,128)(2,1)S(1)}, bf16[128,128]{1,0:T(8,128)(2,1)}, u32[]{:S(2)}) copy-start(bf16[128,128]{1,0:T(8,128)(2,1)} %param.11) | copy-start | bytes 98308
  23.6 48.2 %copy-start.2 = (bf16[128,1024]{1,0:T(8,128)(2,1)S(1)}, bf16[128,1024]{1,0:T(8,128)(2,1)}, u32[]{:S(2)}) copy-start(bf16[128,1024]{1,0:T(8,128)(2,1)} %param.9) | copy-start | bytes 786436
  23.6 416.9 %all-to-all-start = ((bf16[1024,32,128]{2,0,1:T(8,128)(2,1)}), bf16[1024,32,128]{2,0,1:T(8,128)(2,1)}, u32[]{:S(2)}, u32[]{:S(2)}) async-start(bf16[1024,32,128]{2,0,1:T(8,128)(2,1)} %copy.98), calls=%async_computation | async-start | bytes 16777216 | tf_op jit(solution)/shard_map/all_to_all | solution.py:14
  69.9 153.1 %all-gather.2.cloned.1.call-start = ((), (), s32[]{:S(2)}) async-start(), calls=%async_computation.2 | async-start | bytes 2162688 | tf_op jit(solution)/shard_map/all_gather | solution.py:26
Sparse Core Ops, SparseCore 0:
  72.8 150.1 all-gather.1
